TPU v7x, 256 devices: a whole 4x4x8 slice. The times are simulated.
256 devices in a mesh: amp: 256 (over z, y, x, core).
Axes of the slice: x: 4, y: 4, z: 8, core: 2. Of those that a mesh axis runs over, the one named last changes fastest.
Arguments:
- ket_state: float32 [2, 8388608], P(None, 'amp'), may hold values from -6 to 6
- observable: float32 [8388608], P('amp'), may hold values from -6 to 6
- angles: float32 [2, 3], replicated, may hold values from -3.140625 to 3.140625
- gate_kinds: int32 [2, 32], replicated, may hold values from 0 to 2
Outputs:
- bra_state: float32 [2, 8388608], P(None, 'amp')
- grads: float32 [2, 3], replicated
Inputs may be any that keep to these rules, and one draw needn't show every extreme that they name: `gate_kinds`: 0 and 1 name rotations about Y with angles[l, 0] and angles[l, 1], 2 a rotation about Z with angles[l, 2]; entries for qubits at or above the number of qubits are not used.
All inputs are finite; a program needn't handle non-finite values.
Results may differ from a plain program's by a relative error of at most 0.0003.
Values sent between devices are 32-bit elements; how exact they have to be, the bound alone decides.
A program may use at most 128 MiB of HBM per device.

v0:
```python
import functools
import math

import jax
import jax.numpy as jnp
from jax import lax
from jax.experimental import pallas as pl
from jax.experimental.pallas import tpu as pltpu
from jax.sharding import PartitionSpec as P

MESH = pl.DeviceIdType.MESH
QUBITS = 23
LANE_QUBITS = (0, 1, 2, 3, 4, 13, 14)
HOME_ROWS = (7, 8, 9, 10, 11, 12, 5, 6)
AWAY_ROWS = (15, 16, 17, 18, 19, 20, 21, 22)
F32 = jnp.float32


def pair_mask(qubits):
    return sum(1 << q for q in qubits)


ALL_PAIRS = pair_mask(range(QUBITS))
LOCAL_PAIRS = pair_mask(range(14))
AWAY_PAIRS = pair_mask([0] + list(range(13, 23)))
REST_PAIRS = ALL_PAIRS - AWAY_PAIRS


def row_lane():
    row = lax.broadcasted_iota(jnp.int32, (256, 128), 0)
    lane = lax.broadcasted_iota(jnp.int32, (256, 128), 1)
    return row, lane


def entangle(me, away, pairs):
    row, lane = row_lane()
    own = me + jnp.zeros_like(row)
    far, near = (row, own) if away else (own, row)
    index = (lane & 31) | ((near >> 6) << 5) | ((near & 63) << 7) | ((lane >> 5) << 13) | (far << 15)
    both = index & ((index >> 1) | ((index & 1) << 22)) & pairs
    for shift in (16, 8, 4, 2, 1):
        both = both ^ (both >> shift)
    return (1 - 2 * (both & 1)).astype(F32)


def swap_bits(x, row_bit, lane_bit):
    rows = 1 << row_bit
    parts = x.reshape(256 // (2 * rows), 2, rows, 128)
    low, high = parts[:, 0].reshape(128, 128), parts[:, 1].reshape(128, 128)
    step = 1 << lane_bit
    lane = lax.broadcasted_iota(jnp.int32, (128, 128), 1)
    keep = (lane & step) == 0
    new_low = jnp.where(keep, low, pltpu.roll(high, step, 1))
    new_high = jnp.where(keep, pltpu.roll(low, 128 - step, 1), high)
    shape = (256 // (2 * rows), 1, rows, 128)
    return jnp.concatenate([new_low.reshape(shape), new_high.reshape(shape)], axis=1).reshape(256, 128)


def repack(x):
    return swap_bits(swap_bits(x, 6, 5), 7, 6)


def fold8(x):
    return jnp.sum(x.reshape(-1, 8, 128), axis=0)


def bit_sign(axis, position):
    place = lax.broadcasted_iota(jnp.int32, (8, 128), axis)
    return (1 - 2 * ((place >> position) & 1)).astype(F32)


def halves(x, position):
    parts = x.reshape(256 >> (position + 1), 2, 1 << position, 128)
    return parts[:, 0], parts[:, 1]


def flip(x, axis, position):
    step = 1 << position
    if axis == 0:
        y = x.reshape(32, 8, 128)
        place = lax.broadcasted_iota(jnp.int32, (32, 8, 128), 1)
        up, down = pltpu.roll(y, 8 - step, 1), pltpu.roll(y, step, 1)
        return jnp.where((place & step) == 0, up, down).reshape(256, 128)
    place = lax.broadcasted_iota(jnp.int32, (256, 128), 1)
    return jnp.where((place & step) == 0, pltpu.roll(x, 128 - step, 1), pltpu.roll(x, step, 1))


def terms(bra, ket, spots):
    bra_re, bra_im = bra
    ket_re, ket_im = ket
    cross = bra_re * ket_im - bra_im * ket_re
    total = fold8(cross)
    out = []
    for axis, position in spots:
        if axis == 0 and position >= 3:
            br0, br1 = halves(bra_re, position)
            bi0, bi1 = halves(bra_im, position)
            kr0, kr1 = halves(ket_re, position)
            ki0, ki1 = halves(ket_im, position)
            y_part = fold8(br1 * kr0 - br0 * kr1 + bi1 * ki0 - bi0 * ki1)
            c0, c1 = halves(cross, position)
            z_part = fold8(c0 - c1)
        else:
            sign = bit_sign(axis, position)
            pairs = bra_re * flip(ket_re, axis, position) + bra_im * flip(ket_im, axis, position)
            y_part = -sign * fold8(pairs)
            z_part = sign * total
        out.append((y_part, z_part))
    return out


def mm(a, b):
    return lax.dot_general(
        a, b, (((1,), (0,)), ((), ())), precision=lax.Precision.HIGHEST, preferred_element_type=F32
    )


def kernel(
    ket_hbm, obs_hbm, angles, kinds,
    bra_hbm, grads_ref,
    raw, send1, recv1, send2, recv2,
    theta, kind_tab, cos_tab, sy_tab, sz_tab,
    lane1, lane0, home1, home0, away1, away0,
    part, from_z, part_z, from_plane,
    in_sem, out_sem, send_sems, recv_sems,
):
    me = lax.axis_index("amp")
    z, y, x, c = me // 32, (me // 8) % 4, (me // 2) % 4, me % 2
    plane = me % 32
    inner = [((x + dx) % 4) * 2 + (c + dc) % 2 for dx in (2, 1, 3, 0) for dc in (0, 1)]
    tiers = [((y + dy) % 4) * 8 for dy in (2, 1, 3, 0)]

    def to_all(act):
        def body(step, carry):
            dz = jnp.where(step % 2 == 0, 4 + step // 2, 4 - (step + 1) // 2)
            base = ((z + dz) % 8) * 32
            for tier in tiers:
                for spot in inner:
                    act(base + tier + spot)
            return carry

        lax.fori_loop(0, 7, body, 0)
        for t, tier in enumerate(tiers):
            for s, spot in enumerate(inner):
                if (t, s) != (3, 6):
                    act(z * 32 + tier + spot)

    barrier = pltpu.get_barrier_semaphore()
    to_all(lambda d: pl.semaphore_signal(barrier, inc=1, device_id=(d,), device_id_type=MESH))

    loads = [
        pltpu.make_async_copy(ket_hbm.at[:, 0, :], raw.at[0], in_sem.at[0]),
        pltpu.make_async_copy(ket_hbm.at[:, 1, :], raw.at[1], in_sem.at[1]),
        pltpu.make_async_copy(obs_hbm, raw.at[2], in_sem.at[2]),
    ]
    for copy in loads:
        copy.start()

    theta[...] = jnp.zeros_like(theta)
    kind_tab[...] = jnp.zeros_like(kind_tab)
    picks = {}
    for layer in range(2):
        for q in range(QUBITS):
            kind = kinds[layer, q]
            picks[layer, q] = [jnp.where(kind == k, 1.0, 0.0).astype(F32) for k in range(3)]
            angle = jnp.where(
                kind == 0, angles[layer, 0], jnp.where(kind == 1, angles[layer, 1], angles[layer, 2])
            )
            row = layer * 24 + q
            theta[row : row + 1, :] = jnp.full((1, 128), 0.5 * angle, F32)
            kind_tab[row : row + 1, :] = jnp.full((1, 128), kind, jnp.int32)
    cos_tab[...] = jnp.cos(theta[...])
    sines = jnp.sin(theta[...])
    is_z = kind_tab[...] == 2
    sy_tab[...] = jnp.where(is_z, 0.0, sines)
    sz_tab[...] = jnp.where(is_z, sines, 0.0)

    def coefs(layer, q):
        row = slice(layer * 24 + q, layer * 24 + q + 1)
        return cos_tab[row, :], sy_tab[row, :], sz_tab[row, :]

    def kron(out_bits, in_bits, z_bits, layer, qubits, shape):
        real, imag = None, None
        for position, q in enumerate(qubits):
            cosine, sy, sz = coefs(layer, q)
            if shape[1] > 128:
                cosine, sy, sz = (jnp.concatenate([v, v], axis=1) for v in (cosine, sy, sz))
            b_out = (out_bits >> position) & 1
            b_in = (in_bits >> position) & 1
            same = b_out == b_in
            a = jnp.where(same, cosine, sy * (b_in - b_out).astype(F32))
            b = jnp.where(same, sz * (1 - 2 * b_out).astype(F32), 0.0)
            if real is None:
                real, imag = a, b
            else:
                real, imag = real * a - imag * b, real * b + imag * a
        return real, imag

    def build_lane(ref, layer):
        j = lax.broadcasted_iota(jnp.int32, (128, 128), 0)
        k = lax.broadcasted_iota(jnp.int32, (128, 128), 1)
        real, imag = kron(k, j, k, layer, LANE_QUBITS, (128, 128))
        ref[0:128, 0:128] = real
        ref[128:256, 128:256] = real
        ref[0:128, 128:256] = imag
        ref[128:256, 0:128] = -imag

    def build_rows(ref, layer, qubits):
        def body(block, carry):
            j = lax.broadcasted_iota(jnp.int32, (32, 256), 0) + block * 32
            k = lax.broadcasted_iota(jnp.int32, (32, 256), 1)
            real, imag = kron(j, k, j, layer, qubits, (32, 256))
            at = pl.ds(pl.multiple_of(block * 32, 32), 32)
            ref[0, at, :] = real
            ref[1, at, :] = imag
            return carry

        lax.fori_loop(0, 8, body, 0)

    def apply_lanes(x, ref):
        return mm(x, ref[...])

    def apply_rows(x, ref):
        a, b = mm(ref[0], x), mm(ref[1], x)
        return jnp.concatenate([a[:, :128] - b[:, 128:], a[:, 128:] + b[:, :128]], axis=1)

    def split(x):
        return x[:, :128], x[:, 128:]

    for copy in loads:
        copy.wait()
    for i in range(3):
        send1[i] = repack(raw[i])
    recv1[:, pl.ds(me, 1), :] = send1[:, pl.ds(me, 1), :]

    build_lane(lane1, 1)
    build_rows(home1, 1, HOME_ROWS)

    pl.semaphore_wait(barrier, 255)

    def exchange(source, target, slot):
        def act(d):
            pltpu.make_async_remote_copy(
                src_ref=source.at[:, pl.ds(d, 1), :],
                dst_ref=target.at[:, pl.ds(me, 1), :],
                send_sem=send_sems.at[slot],
                recv_sem=recv_sems.at[slot],
                device_id=(d,),
                device_id_type=MESH,
            ).start()

        to_all(act)
        return pltpu.make_async_remote_copy(
            src_ref=source.at[:, pl.ds(0, 255), :],
            dst_ref=target.at[:, pl.ds(0, 255), :],
            send_sem=send_sems.at[slot],
            recv_sem=recv_sems.at[slot],
            device_id=(me,),
            device_id_type=MESH,
        )

    first = exchange(send1, recv1, 0)

    scale = 2.0 / math.sqrt(1 << QUBITS)

    def start_state(ref, sign):
        ket_re, ket_im = ref[0] * sign, ref[1] * sign
        obs = ref[2] * scale
        return (obs * ket_re, obs * ket_im), (ket_re, ket_im)

    acc = {(layer, k): jnp.zeros((8, 128), F32) for layer in range(2) for k in range(3)}

    def tally(layer, qubits, values):
        for q, (y_part, z_part) in zip(qubits, values):
            pick = picks[layer, q]
            acc[layer, 0] = acc[layer, 0] + pick[0] * y_part
            acc[layer, 1] = acc[layer, 1] + pick[1] * y_part
            acc[layer, 2] = acc[layer, 2] + pick[2] * z_part

    spots = [(1, p) for p in range(7)] + [(0, p) for p in range(8)]
    local = list(LANE_QUBITS) + list(HOME_ROWS)
    bra, ket = start_state(send1, entangle(me, False, ALL_PAIRS))
    tally(1, local, terms(bra, ket, spots))
    local_sign = entangle(me, False, LOCAL_PAIRS)
    sign2 = jnp.concatenate([local_sign, local_sign], axis=1)

    def layer_one(state, rows_ref, sign2):
        x = jnp.concatenate(state, axis=1)
        return apply_rows(apply_lanes(x, lane1), rows_ref) * sign2

    bra1 = split(layer_one(bra, home1, sign2))
    ket1 = split(layer_one(ket, home1, sign2))
    inside = [(q, s) for q, s in zip(local, spots) if q not in (0, 14)]
    tally(0, [q for q, _ in inside], terms(bra1, ket1, [s for _, s in inside]))

    build_rows(away1, 1, AWAY_ROWS)
    build_rows(away0, 0, AWAY_ROWS)
    away_sign = entangle(me, True, AWAY_PAIRS)
    away2 = jnp.concatenate([away_sign, away_sign], axis=1)

    first.wait_recv()

    bra, ket = start_state(recv1, entangle(me, True, ALL_PAIRS))
    bra_x = layer_one(bra, away1, away2)
    done = apply_rows(bra_x, away0)
    send2[0], send2[1] = split(done)
    recv2[:, pl.ds(me, 1), :] = send2[:, pl.ds(me, 1), :]
    second = exchange(send2, recv2, 1)

    tally(1, AWAY_ROWS, terms(bra, ket, [(0, p) for p in range(8)]))
    ket_x = layer_one(ket, away1, away2)
    tally(
        0,
        list(AWAY_ROWS) + [0, 14],
        terms(split(bra_x), split(ket_x), [(0, p) for p in range(8)] + [(1, 0), (1, 6)]),
    )

    lane8 = lax.broadcasted_iota(jnp.int32, (8, 128), 1)
    mine = jnp.zeros((8, 128), F32)
    for layer in range(2):
        for k in range(3):
            value = 0.5 * jnp.sum(acc[layer, k], keepdims=True)
            mine = mine + jnp.where(lane8 == 3 * layer + k, value, 0.0)
    part[...] = mine
    from_z[pl.ds(z, 1)] = mine[None]
    peers_z = [((z + dz) % 8) * 32 + plane for dz in (4, 3, 5, 2, 6, 1, 7)]
    for d in peers_z:
        pltpu.make_async_remote_copy(
            src_ref=part, dst_ref=from_z.at[z], send_sem=send_sems.at[2], recv_sem=recv_sems.at[2],
            device_id=(d,), device_id_type=MESH,
        ).start()

    build_lane(lane0, 0)
    build_rows(home0, 0, HOME_ROWS)
    rest_sign = entangle(me, False, REST_PAIRS)
    rest2 = jnp.concatenate([rest_sign, rest_sign], axis=1)

    third = pltpu.make_async_remote_copy(
        src_ref=from_z.at[pl.ds(0, 7)], dst_ref=from_z.at[pl.ds(0, 7)],
        send_sem=send_sems.at[2], recv_sem=recv_sems.at[2], device_id=(me,), device_id_type=MESH,
    )
    third.wait_recv()
    summed = jnp.sum(from_z[...], axis=0)
    part_z[...] = summed
    from_plane[pl.ds(plane, 1)] = summed[None]
    for t, tier in enumerate(tiers):
        for s, spot in enumerate(inner):
            if (t, s) != (3, 6):
                pltpu.make_async_remote_copy(
                    src_ref=part_z, dst_ref=from_plane.at[plane],
                    send_sem=send_sems.at[3], recv_sem=recv_sems.at[3],
                    device_id=(z * 32 + tier + spot,), device_id_type=MESH,
                ).start()
    fourth = pltpu.make_async_remote_copy(
        src_ref=from_plane.at[pl.ds(0, 31)], dst_ref=from_plane.at[pl.ds(0, 31)],
        send_sem=send_sems.at[3], recv_sem=recv_sems.at[3], device_id=(me,), device_id_type=MESH,
    )

    second.wait_recv()
    x2 = jnp.concatenate([recv2[0], recv2[1]], axis=1)
    x2 = apply_rows(x2, home1) * rest2
    x2 = apply_rows(apply_lanes(x2, lane0), home0)
    re, im = split(x2)
    raw[0] = repack(re)
    raw[1] = repack(im)
    stores = [
        pltpu.make_async_copy(raw.at[0], bra_hbm.at[:, 0, :], out_sem.at[0]),
        pltpu.make_async_copy(raw.at[1], bra_hbm.at[:, 1, :], out_sem.at[1]),
    ]
    for copy in stores:
        copy.start()

    fourth.wait_recv()
    total = jnp.sum(from_plane[...], axis=0)
    grads_ref[...] = jnp.concatenate([total[0:1, 0:3], total[0:1, 3:6]], axis=0)
    for copy in (first, second, third, fourth):
        copy.wait_send()
    for copy in stores:
        copy.wait()


def on_device(ket_state, observable, angles, gate_kinds):
    ket = ket_state.reshape(2, 256, 128).transpose(1, 0, 2)
    obs = observable.reshape(256, 128)
    anywhere = pl.BlockSpec(memory_space=pl.ANY)
    scalars = pl.BlockSpec(memory_space=pltpu.SMEM)
    vmem = lambda *shape, dtype=F32: pltpu.VMEM(shape, dtype)
    bra, grads = pl.pallas_call(
        kernel,
        out_shape=(
            jax.ShapeDtypeStruct((256, 2, 128), F32),
            jax.ShapeDtypeStruct((2, 3), F32),
        ),
        in_specs=[anywhere, anywhere, scalars, scalars],
        out_specs=(anywhere, pl.BlockSpec(memory_space=pltpu.VMEM)),
        scratch_shapes=[
            vmem(3, 256, 128), vmem(3, 256, 128), vmem(3, 256, 128),
            vmem(2, 256, 128), vmem(2, 256, 128),
            vmem(48, 128), vmem(48, 128, dtype=jnp.int32),
            vmem(48, 128), vmem(48, 128), vmem(48, 128),
            vmem(256, 256), vmem(256, 256),
            vmem(2, 256, 256), vmem(2, 256, 256), vmem(2, 256, 256), vmem(2, 256, 256),
            vmem(8, 128), vmem(8, 8, 128), vmem(8, 128), vmem(32, 8, 128),
            pltpu.SemaphoreType.DMA((3,)), pltpu.SemaphoreType.DMA((2,)),
            pltpu.SemaphoreType.DMA((4,)), pltpu.SemaphoreType.DMA((4,)),
        ],
        compiler_params=pltpu.CompilerParams(collective_id=0, has_side_effects=True),
    )(ket, obs, angles, gate_kinds)
    return bra.transpose(1, 0, 2).reshape(2, 32768), grads


def solution(mesh):
    return jax.shard_map(
        on_device,
        mesh=mesh,
        in_specs=(P(None, "amp"), P("amp"), P(), P()),
        out_specs=(P(None, "amp"), P()),
        check_vma=False,
    )
```

profile of v0, /device:TPU:1, one launch (start us, length us, event | category | flops | bytes accessed | tf_op | source)
XLA Modules:
  0.0 47.1 jit_solution(13641625020058445877)
XLA Ops:
  0.6 44.2 %shard_map.59 = (f32[256,2,128]{2,1,0:T(2,128)}, f32[2,3]{1,0:T(2,128)}) custom-call(f32[256,2,128]{2,1,0:T(2,128)} %bitcast.7, f32[256,128]{1,0:T(8,128)} %bitcast.9, f32[2,3]{1,0:T(2,128)} %angles.1, s32[2,32]{1,0:T(2,128)} %kinds.1), custom_call_target="tpu_custom_call" | custom-call | tf_op jit(solution)/shard_map/pallas_call | solution.py:388
  44.9 0.0 copy-start
  44.9 1.7 %copy.8 = f32[2,32768]{1,0:T(2,128)} copy(f32[2,32768]{1,0:T(2,128)} %bitcast.8) | data formatting | bytes 524288
  46.5 0.0 copy-done
  46.6 0.6 %copy.9 = f32[2,3]{1,0:T(2,128)} copy(f32[2,3]{1,0:T(2,128)S(1)} %copy-done) | data formatting | bytes 48
Async XLA Ops:
  44.9 1.7 %copy-start = (f32[2,3]{1,0:T(2,128)S(1)}, f32[2,3]{1,0:T(2,128)}, u32[]{:S(2)}) copy-start(f32[2,3]{1,0:T(2,128)} %get-tuple-element.9) | copy-start | bytes 76
where the time goes:
time: 47.3 us; the launch traced here: 47.1 us
  Pallas kernels  44.2 us (93%)
  local copies, waits for them, and re-layouts  2.24 us (5%)
  between operations  0.65 us (1%)
    pallas_call x1, Pallas kernels, on_device(): pl.pallas_call(kernel, out_shape=(jax.ShapeDtypeStruct((256, 2, 128), F32...  44.2 us
    unnamed x4, local copies, waits for them, and re-layouts  2.24 us

commit v1 on v0

v1 whole, which is shorter than its diff:
```python
import functools
import math

import jax
import jax.numpy as jnp
from jax import lax
from jax.experimental import pallas as pl
from jax.experimental.pallas import tpu as pltpu
from jax.sharding import PartitionSpec as P

MESH = pl.DeviceIdType.MESH
QUBITS = 23
LANE_QUBITS = (0, 1, 2, 3, 4, 13, 14)
HOME_ROWS = (7, 8, 9, 10, 11, 12, 5, 6)
AWAY_ROWS = (15, 16, 17, 18, 19, 20, 21, 22)
F32 = jnp.float32


def pair_mask(qubits):
    return sum(1 << q for q in qubits)


ALL_PAIRS = pair_mask(range(QUBITS))
LOCAL_PAIRS = pair_mask(range(14))
AWAY_PAIRS = pair_mask([0] + list(range(13, 23)))
REST_PAIRS = ALL_PAIRS - AWAY_PAIRS


def row_lane():
    row = lax.broadcasted_iota(jnp.int32, (256, 128), 0)
    lane = lax.broadcasted_iota(jnp.int32, (256, 128), 1)
    return row, lane


def entangle(me, away, pairs):
    row, lane = row_lane()
    own = me + jnp.zeros_like(row)
    far, near = (row, own) if away else (own, row)
    index = (lane & 31) | ((near >> 6) << 5) | ((near & 63) << 7) | ((lane >> 5) << 13) | (far << 15)
    both = index & ((index >> 1) | ((index & 1) << 22)) & pairs
    for shift in (16, 8, 4, 2, 1):
        both = both ^ (both >> shift)
    return (1 - 2 * (both & 1)).astype(F32)


def swap_bits(x, row_bit, lane_bit):
    rows = 1 << row_bit
    parts = x.reshape(256 // (2 * rows), 2, rows, 128)
    low, high = parts[:, 0].reshape(128, 128), parts[:, 1].reshape(128, 128)
    step = 1 << lane_bit
    lane = lax.broadcasted_iota(jnp.int32, (128, 128), 1)
    keep = (lane & step) == 0
    new_low = jnp.where(keep, low, pltpu.roll(high, step, 1))
    new_high = jnp.where(keep, pltpu.roll(low, 128 - step, 1), high)
    shape = (256 // (2 * rows), 1, rows, 128)
    return jnp.concatenate([new_low.reshape(shape), new_high.reshape(shape)], axis=1).reshape(256, 128)


def repack(x):
    return swap_bits(swap_bits(x, 6, 5), 7, 6)


def fold8(x):
    return jnp.sum(x.reshape(-1, 8, 128), axis=0)


def bit_sign(axis, position):
    place = lax.broadcasted_iota(jnp.int32, (8, 128), axis)
    return (1 - 2 * ((place >> position) & 1)).astype(F32)


def halves(x, position):
    parts = x.reshape(256 >> (position + 1), 2, 1 << position, 128)
    return parts[:, 0], parts[:, 1]


def flip(x, axis, position):
    step = 1 << position
    if axis == 0:
        y = x.reshape(32, 8, 128)
        place = lax.broadcasted_iota(jnp.int32, (32, 8, 128), 1)
        up, down = pltpu.roll(y, 8 - step, 1), pltpu.roll(y, step, 1)
        return jnp.where((place & step) == 0, up, down).reshape(256, 128)
    place = lax.broadcasted_iota(jnp.int32, (256, 128), 1)
    return jnp.where((place & step) == 0, pltpu.roll(x, 128 - step, 1), pltpu.roll(x, step, 1))


def terms(bra, ket, spots):
    bra_re, bra_im = bra
    ket_re, ket_im = ket
    cross = bra_re * ket_im - bra_im * ket_re
    total = fold8(cross)
    out = []
    for axis, position in spots:
        if axis == 0 and position >= 3:
            br0, br1 = halves(bra_re, position)
            bi0, bi1 = halves(bra_im, position)
            kr0, kr1 = halves(ket_re, position)
            ki0, ki1 = halves(ket_im, position)
            y_part = fold8(br1 * kr0 - br0 * kr1 + bi1 * ki0 - bi0 * ki1)
            c0, c1 = halves(cross, position)
            z_part = fold8(c0 - c1)
        else:
            sign = bit_sign(axis, position)
            pairs = bra_re * flip(ket_re, axis, position) + bra_im * flip(ket_im, axis, position)
            y_part = -sign * fold8(pairs)
            z_part = sign * total
        out.append((y_part, z_part))
    return out


def cut(x):
    high = x.astype(jnp.bfloat16)
    return high, (x - high.astype(F32)).astype(jnp.bfloat16)


def mm(a, b):
    (a_high, a_low), (b_high, b_low) = a, b
    dot = functools.partial(jnp.dot, preferred_element_type=F32)
    return dot(a_high, b_high) + (dot(a_high, b_low) + dot(a_low, b_high))


def kernel(
    ket_hbm, obs_hbm, angles_hbm, kinds_hbm,
    bra_ref, grads_ref,
    angles, kinds, raw, send1, recv1, send2, recv2,
    theta, kind_tab, cos_tab, sy_tab, sz_tab,
    lane1, lane0, home1, home0, away1, away0,
    part, from_z, part_z, from_plane,
    in_sem, send_sems, recv_sems,
):
    me = lax.axis_index("amp")
    z, y, x, c = me // 32, (me // 8) % 4, (me // 2) % 4, me % 2
    plane = me % 32
    inner = [((x + dx) % 4) * 2 + (c + dc) % 2 for dx in (2, 1, 3, 0) for dc in (0, 1)]
    tiers = [((y + dy) % 4) * 8 for dy in (2, 1, 3, 0)]

    def to_all(act, begin=0, end=8):
        def body(step, carry):
            dz = jnp.where(step % 2 == 0, 4 + step // 2, 4 - (step + 1) // 2)
            base = ((z + dz) % 8) * 32
            for tier in tiers:
                for spot in inner:
                    act(base + tier + spot)
            return carry

        lax.fori_loop(begin, min(end, 7), body, 0)
        if end == 8:
            to_plane(lambda d, spot: act(d))

    def to_plane(act):
        for t, tier in enumerate(tiers):
            for s, spot in enumerate(inner):
                if (t, s) != (3, 6):
                    act(z * 32 + tier + spot, tier + spot)

    barrier = pltpu.get_barrier_semaphore()
    to_all(lambda d: pl.semaphore_signal(barrier, inc=1, device_id=(d,), device_id_type=MESH))

    loads = [
        pltpu.make_async_copy(ket_hbm.at[:, 0, :], raw.at[0], in_sem.at[0]),
        pltpu.make_async_copy(ket_hbm.at[:, 1, :], raw.at[1], in_sem.at[1]),
        pltpu.make_async_copy(obs_hbm, raw.at[2], in_sem.at[2]),
    ]
    settings = [
        pltpu.make_async_copy(angles_hbm, angles, in_sem.at[3]),
        pltpu.make_async_copy(kinds_hbm, kinds, in_sem.at[4]),
    ]
    for copy in loads + settings:
        copy.start()

    def coefs(layer, q):
        row = slice(layer * 24 + q, layer * 24 + q + 1)
        return cos_tab[row, :], sy_tab[row, :], sz_tab[row, :]

    def kron(out_bits, in_bits, z_bits, layer, qubits, shape):
        real, imag = None, None
        for position, q in enumerate(qubits):
            cosine, sy, sz = coefs(layer, q)
            if shape[1] > 128:
                cosine, sy, sz = (jnp.concatenate([v, v], axis=1) for v in (cosine, sy, sz))
            b_out = (out_bits >> position) & 1
            b_in = (in_bits >> position) & 1
            same = b_out == b_in
            a = jnp.where(same, cosine, sy * (b_in - b_out).astype(F32))
            b = jnp.where(same, sz * (1 - 2 * b_out).astype(F32), 0.0)
            if real is None:
                real, imag = a, b
            else:
                real, imag = real * a - imag * b, real * b + imag * a
        return real, imag

    def build_lane(ref, layer):
        j = lax.broadcasted_iota(jnp.int32, (128, 128), 0)
        k = lax.broadcasted_iota(jnp.int32, (128, 128), 1)
        real, imag = kron(k, j, k, layer, LANE_QUBITS, (128, 128))
        for i, (re, im) in enumerate(zip(cut(real), cut(imag))):
            ref[i, 0:128, 0:128] = re
            ref[i, 128:256, 128:256] = re
            ref[i, 0:128, 128:256] = im
            ref[i, 128:256, 0:128] = -im

    def build_rows(ref, layer, qubits):
        def body(block, carry):
            j = lax.broadcasted_iota(jnp.int32, (32, 256), 0) + block * 32
            k = lax.broadcasted_iota(jnp.int32, (32, 256), 1)
            real, imag = kron(j, k, j, layer, qubits, (32, 256))
            at = pl.ds(pl.multiple_of(block * 32, 32), 32)
            for i, (re, im) in enumerate(zip(cut(real), cut(imag))):
                ref[0, i, at, :] = re
                ref[1, i, at, :] = im
            return carry

        lax.fori_loop(0, 8, body, 0)

    def apply_lanes(x, ref):
        return mm(cut(x), (ref[0], ref[1]))

    def apply_rows(x, ref):
        x = cut(x)
        a, b = mm((ref[0, 0], ref[0, 1]), x), mm((ref[1, 0], ref[1, 1]), x)
        return jnp.concatenate([a[:, :128] - b[:, 128:], a[:, 128:] + b[:, :128]], axis=1)

    def split(x):
        return x[:, :128], x[:, 128:]

    for copy in loads:
        copy.wait()
    for i in range(3):
        send1[i] = repack(raw[i])
    recv1[:, pl.ds(me, 1), :] = send1[:, pl.ds(me, 1), :]

    pl.semaphore_wait(barrier, 255)

    def exchange(source, target, slot, begin=0, end=8):
        def act(d):
            pltpu.make_async_remote_copy(
                src_ref=source.at[:, pl.ds(d, 1), :],
                dst_ref=target.at[:, pl.ds(me, 1), :],
                send_sem=send_sems.at[slot],
                recv_sem=recv_sems.at[slot],
                device_id=(d,),
                device_id_type=MESH,
            ).start()

        to_all(act, begin, end)

    def exchanged(source, target, slot):
        return pltpu.make_async_remote_copy(
            src_ref=source.at[:, pl.ds(0, 255), :],
            dst_ref=target.at[:, pl.ds(0, 255), :],
            send_sem=send_sems.at[slot],
            recv_sem=recv_sems.at[slot],
            device_id=(me,),
            device_id_type=MESH,
        )

    exchange(send1, recv1, 0)
    first = exchanged(send1, recv1, 0)

    for copy in settings:
        copy.wait()
    theta[...] = jnp.zeros_like(theta)
    kind_tab[...] = jnp.zeros_like(kind_tab)
    picks = {}
    for layer in range(2):
        for q in range(QUBITS):
            kind = kinds[layer, q]
            picks[layer, q] = [jnp.where(kind == k, 1.0, 0.0).astype(F32) for k in range(3)]
            angle = jnp.where(
                kind == 0, angles[layer, 0], jnp.where(kind == 1, angles[layer, 1], angles[layer, 2])
            )
            row = layer * 24 + q
            theta[row : row + 1, :] = jnp.full((1, 128), 0.5 * angle, F32)
            kind_tab[row : row + 1, :] = jnp.full((1, 128), kind, jnp.int32)
    cos_tab[...] = jnp.cos(theta[...])
    sines = jnp.sin(theta[...])
    is_z = kind_tab[...] == 2
    sy_tab[...] = jnp.where(is_z, 0.0, sines)
    sz_tab[...] = jnp.where(is_z, sines, 0.0)

    build_lane(lane1, 1)
    build_rows(away1, 1, AWAY_ROWS)
    build_rows(away0, 0, AWAY_ROWS)
    build_rows(home1, 1, HOME_ROWS)

    scale = 2.0 / math.sqrt(1 << QUBITS)

    def start_state(ref, sign):
        ket_re, ket_im = ref[0] * sign, ref[1] * sign
        obs = ref[2] * scale
        return (obs * ket_re, obs * ket_im), (ket_re, ket_im)

    acc = {(layer, k): jnp.zeros((8, 128), F32) for layer in range(2) for k in range(3)}

    def tally(layer, qubits, values):
        for q, (y_part, z_part) in zip(qubits, values):
            pick = picks[layer, q]
            acc[layer, 0] = acc[layer, 0] + pick[0] * y_part
            acc[layer, 1] = acc[layer, 1] + pick[1] * y_part
            acc[layer, 2] = acc[layer, 2] + pick[2] * z_part

    spots = [(1, p) for p in range(7)] + [(0, p) for p in range(8)]
    local = list(LANE_QUBITS) + list(HOME_ROWS)
    bra, ket = start_state(send1, entangle(me, False, ALL_PAIRS))
    tally(1, local, terms(bra, ket, spots))
    local_sign = entangle(me, False, LOCAL_PAIRS)
    sign2 = jnp.concatenate([local_sign, local_sign], axis=1)

    def layer_one(state, rows_ref, sign2):
        x = jnp.concatenate(state, axis=1)
        return apply_rows(apply_lanes(x, lane1), rows_ref) * sign2

    bra1 = split(layer_one(bra, home1, sign2))
    ket1 = split(layer_one(ket, home1, sign2))
    inside = [(q, s) for q, s in zip(local, spots) if q not in (0, 14)]
    tally(0, [q for q, _ in inside], terms(bra1, ket1, [s for _, s in inside]))

    build_lane(lane0, 0)
    build_rows(home0, 0, HOME_ROWS)
    away_sign = entangle(me, True, AWAY_PAIRS)
    away2 = jnp.concatenate([away_sign, away_sign], axis=1)

    first.wait_recv()

    bra, ket = start_state(recv1, entangle(me, True, ALL_PAIRS))
    bra_x = layer_one(bra, away1, away2)
    done = apply_rows(bra_x, away0)
    send2[0], send2[1] = split(done)
    recv2[:, pl.ds(me, 1), :] = send2[:, pl.ds(me, 1), :]
    exchange(send2, recv2, 1, 0, 4)

    tally(1, AWAY_ROWS, terms(bra, ket, [(0, p) for p in range(8)]))
    ket_x = layer_one(ket, away1, away2)
    tally(
        0,
        list(AWAY_ROWS) + [0, 14],
        terms(split(bra_x), split(ket_x), [(0, p) for p in range(8)] + [(1, 0), (1, 6)]),
    )

    lane8 = lax.broadcasted_iota(jnp.int32, (8, 128), 1)
    mine = jnp.zeros((8, 128), F32)
    for layer in range(2):
        for k in range(3):
            value = 0.5 * jnp.sum(acc[layer, k], keepdims=True)
            mine = mine + jnp.where(lane8 == 3 * layer + k, value, 0.0)
    part[...] = mine
    from_plane[pl.ds(plane, 1)] = mine[None]

    def hand_over(d, spot):
        pltpu.make_async_remote_copy(
            src_ref=part, dst_ref=from_plane.at[plane], send_sem=send_sems.at[2], recv_sem=recv_sems.at[2],
            device_id=(d,), device_id_type=MESH,
        ).start()

    to_plane(hand_over)
    third = pltpu.make_async_remote_copy(
        src_ref=from_plane.at[pl.ds(0, 31)], dst_ref=from_plane.at[pl.ds(0, 31)],
        send_sem=send_sems.at[2], recv_sem=recv_sems.at[2], device_id=(me,), device_id_type=MESH,
    )
    exchange(send2, recv2, 1, 4, 8)
    second = exchanged(send2, recv2, 1)
    rest_sign = entangle(me, False, REST_PAIRS)
    rest2 = jnp.concatenate([rest_sign, rest_sign], axis=1)

    third.wait_recv()
    summed = jnp.sum(from_plane[...], axis=0)
    part_z[...] = summed
    from_z[pl.ds(z, 1)] = summed[None]
    for dz in (4, 3, 5, 2, 6, 1, 7):
        pltpu.make_async_remote_copy(
            src_ref=part_z, dst_ref=from_z.at[z], send_sem=send_sems.at[3], recv_sem=recv_sems.at[3],
            device_id=(((z + dz) % 8) * 32 + plane,), device_id_type=MESH,
        ).start()
    fourth = pltpu.make_async_remote_copy(
        src_ref=from_z.at[pl.ds(0, 7)], dst_ref=from_z.at[pl.ds(0, 7)],
        send_sem=send_sems.at[3], recv_sem=recv_sems.at[3], device_id=(me,), device_id_type=MESH,
    )

    second.wait_recv()
    x2 = jnp.concatenate([recv2[0], recv2[1]], axis=1)
    x2 = apply_rows(x2, home1) * rest2
    x2 = apply_rows(apply_lanes(x2, lane0), home0)
    bra_ref[0], bra_ref[1] = split(x2)

    fourth.wait_recv()
    grads_ref[...] = jnp.sum(from_z[...], axis=0)
    for copy in (first, second, third, fourth):
        copy.wait_send()


def finish(state, sums, bra_hbm, grads_ref, raw, out_sem):
    stores = []
    for i in range(2):
        raw[i] = repack(state[i])
        stores.append(pltpu.make_async_copy(raw.at[i], bra_hbm.at[:, i, :], out_sem.at[i]))
        stores[i].start()
    total = sums[0:1, :]
    grads_ref[...] = jnp.concatenate([total[:, 0:3], total[:, 3:6]], axis=0)
    for copy in stores:
        copy.wait()


def on_device(ket_state, observable, angles, gate_kinds):
    ket = ket_state.reshape(2, 256, 128).transpose(1, 0, 2)
    obs = observable.reshape(256, 128)
    main_memory = pl.BlockSpec(memory_space=pltpu.HBM)
    vmem = lambda *shape, dtype=F32: pltpu.VMEM(shape, dtype)
    half = lambda *shape: pltpu.VMEM(shape, jnp.bfloat16)
    on_chip = pl.BlockSpec(memory_space=pltpu.VMEM)
    state, sums = pl.pallas_call(
        kernel,
        out_shape=(
            jax.ShapeDtypeStruct((2, 256, 128), F32),
            jax.ShapeDtypeStruct((8, 128), F32),
        ),
        in_specs=[main_memory] * 4,
        out_specs=(on_chip, on_chip),
        scratch_shapes=[
            pltpu.SMEM((2, 3), F32), pltpu.SMEM((2, 32), jnp.int32),
            vmem(3, 256, 128), vmem(3, 256, 128), vmem(3, 256, 128),
            vmem(2, 256, 128), vmem(2, 256, 128),
            vmem(48, 128), vmem(48, 128, dtype=jnp.int32),
            vmem(48, 128), vmem(48, 128), vmem(48, 128),
            half(2, 256, 256), half(2, 256, 256),
            half(2, 2, 256, 256), half(2, 2, 256, 256), half(2, 2, 256, 256), half(2, 2, 256, 256),
            vmem(8, 128), vmem(8, 8, 128), vmem(8, 128), vmem(32, 8, 128),
            pltpu.SemaphoreType.DMA((5,)),
            pltpu.SemaphoreType.DMA((4,)), pltpu.SemaphoreType.DMA((4,)),
        ],
        compiler_params=pltpu.CompilerParams(
            collective_id=0, has_side_effects=True, vmem_limit_bytes=16 << 20
        ),
    )(*(pltpu.with_memory_space_constraint(v, pltpu.HBM) for v in (ket, obs, angles, gate_kinds)))
    bra, grads = pl.pallas_call(
        finish,
        out_shape=(
            jax.ShapeDtypeStruct((256, 2, 128), F32),
            jax.ShapeDtypeStruct((2, 3), F32),
        ),
        in_specs=[on_chip, on_chip],
        out_specs=(main_memory, on_chip),
        scratch_shapes=[vmem(2, 256, 128), pltpu.SemaphoreType.DMA((2,))],
        compiler_params=pltpu.CompilerParams(vmem_limit_bytes=4 << 20),
    )(state, sums)
    return bra.transpose(1, 0, 2).reshape(2, 32768), grads


def solution(mesh):
    return jax.shard_map(
        on_device,
        mesh=mesh,
        in_specs=(P(None, "amp"), P("amp"), P(), P()),
        out_specs=(P(None, "amp"), P()),
        check_vma=False,
    )
```

time: 47.3 us -> 41.6 us (0.88)
  Pallas kernels: 44.2 us -> 40.9 us
  local copies, waits for them, and re-layouts: 2.24 us -> 0 us
    pallas_call x1 -> x2, Pallas kernels: 44.2 us -> 40.9 us  [the longest x1 39.3 us: on_device(): pl.pallas_call(kernel, out_shape=(jax.ShapeDtypeStruct((2, 256, 128), F32...]
    unnamed x4 -> x0, local copies, waits for them, and re-layouts: 2.24 us -> none
where the time goes in v1:
time: 41.6 us; the launch traced here: 41.5 us
  Pallas kernels  40.9 us (98%)
  between operations  0.64 us (2%)
    pallas_call x1, Pallas kernels, on_device(): pl.pallas_call(kernel, out_shape=(jax.ShapeDtypeStruct((2, 256, 128), F32...  39.3 us
    pallas_call x1, Pallas kernels, on_device(): pl.pallas_call(finish, out_shape=(jax.ShapeDtypeStruct((256, 2, 128), F32...  1.54 us

profile of v1, /device:TPU:1, one launch (start us, length us, event | category | flops | bytes accessed | tf_op | source)
XLA Modules:
  0.0 41.5 jit_solution(16249778820181775786)
XLA Ops:
  0.6 39.3 %shard_map.59 = (f32[2,256,128]{2,1,0:T(8,128)S(1)}, f32[8,128]{1,0:T(8,128)S(1)}) custom-call(f32[256,2,128]{2,1,0:T(2,128)} %bitcast.7, f32[256,128]{1,0:T(8,128)} %bitcast.8, f32[2,3]{1,0:T(2,128)} %angles_hbm.1, s32[2,32]{1,0:T(2,128)} %kinds_hbm.1), custom_call_target="tpu_custom_call" | custom-call | tf_op jit(solution)/shard_map/pallas_call | solution.py:411
  40.0 1.5 %shard_map.60 = (f32[256,2,128]{2,1,0:T(2,128)}, f32[2,3]{1,0:T(2,128)}) custom-call(f32[2,256,128]{2,1,0:T(8,128)S(1)} %get-tuple-element.6.state, f32[8,128]{1,0:T(8,128)S(1)} %get-tuple-element.7.sums), custom_call_target="tpu_custom_call" | custom-call | tf_op jit(solution)/shard_map/pallas_call | solution.py:435

commit v2 on v1

--- a/solution.py
+++ b/solution.py
@@ -32,11 +32,12 @@
     return row, lane
 
 
-def entangle(me, away, pairs):
+def entangle(me, pairs, chunk=None):
     row, lane = row_lane()
     own = me + jnp.zeros_like(row)
-    far, near = (row, own) if away else (own, row)
-    index = (lane & 31) | ((near >> 6) << 5) | ((near & 63) << 7) | ((lane >> 5) << 13) | (far << 15)
+    far, near = (own, row) if chunk is None else (row, own)
+    low = lane & 31 if chunk is None else (lane & 15) | (chunk << 4)
+    index = low | ((near >> 6) << 5) | ((near & 63) << 7) | ((lane >> 5) << 13) | (far << 15)
     both = index & ((index >> 1) | ((index & 1) << 22)) & pairs
     for shift in (16, 8, 4, 2, 1):
         both = both ^ (both >> shift)
@@ -60,6 +61,32 @@
     return swap_bits(swap_bits(x, 6, 5), 7, 6)
 
 
+def lane_bit4():
+    return (lax.broadcasted_iota(jnp.int32, (256, 128), 1) & 16) == 0
+
+
+def up(x):
+    return pltpu.roll(x, 16, 1)
+
+
+def down(x):
+    return pltpu.roll(x, 112, 1)
+
+
+def to_chunks(real, imag):
+    keep = lane_bit4()
+    return jnp.where(keep, real, up(imag)), jnp.where(keep, down(real), imag)
+
+
+def from_chunks(first, second):
+    keep = lane_bit4()
+    return jnp.where(keep, first, up(second)), jnp.where(keep, down(first), second)
+
+
+def times_i(x):
+    return jnp.where(lane_bit4(), -down(x), up(x))
+
+
 def fold8(x):
     return jnp.sum(x.reshape(-1, 8, 128), axis=0)
 
@@ -85,30 +112,38 @@
     return jnp.where((place & step) == 0, pltpu.roll(x, 128 - step, 1), pltpu.roll(x, step, 1))
 
 
-def terms(bra, ket, spots):
-    bra_re, bra_im = bra
-    ket_re, ket_im = ket
-    cross = bra_re * ket_im - bra_im * ket_re
+def terms(bras, kets, cross, spots):
     total = fold8(cross)
     out = []
     for axis, position in spots:
         if axis == 0 and position >= 3:
-            br0, br1 = halves(bra_re, position)
-            bi0, bi1 = halves(bra_im, position)
-            kr0, kr1 = halves(ket_re, position)
-            ki0, ki1 = halves(ket_im, position)
-            y_part = fold8(br1 * kr0 - br0 * kr1 + bi1 * ki0 - bi0 * ki1)
+            y_part = 0.0
+            for bra, ket in zip(bras, kets):
+                b0, b1 = halves(bra, position)
+                k0, k1 = halves(ket, position)
+                y_part = y_part + (b1 * k0 - b0 * k1)
+            y_part = fold8(y_part)
             c0, c1 = halves(cross, position)
             z_part = fold8(c0 - c1)
         else:
             sign = bit_sign(axis, position)
-            pairs = bra_re * flip(ket_re, axis, position) + bra_im * flip(ket_im, axis, position)
+            pairs = sum(bra * flip(ket, axis, position) for bra, ket in zip(bras, kets))
             y_part = -sign * fold8(pairs)
             z_part = sign * total
         out.append((y_part, z_part))
     return out
 
 
+def chunk_terms(bra, ket, spots):
+    turned = flip(ket, 1, 4)
+    cross = bra * jnp.where(lane_bit4(), turned, -turned)
+    return terms([bra], [ket], cross, spots)
+
+
+def home_terms(bra, ket, spots):
+    return terms(bra, ket, bra[0] * ket[1] - bra[1] * ket[0], spots)
+
+
 def cut(x):
     high = x.astype(jnp.bfloat16)
     return high, (x - high.astype(F32)).astype(jnp.bfloat16)
@@ -123,9 +158,9 @@
 def kernel(
     ket_hbm, obs_hbm, angles_hbm, kinds_hbm,
     bra_ref, grads_ref,
-    angles, kinds, raw, send1, recv1, send2, recv2,
+    angles, kinds, raw, send_a, send_b, recv_a, recv_b, send_c, send_d, recv_c, recv_d,
     theta, kind_tab, cos_tab, sy_tab, sz_tab,
-    lane1, lane0, home1, home0, away1, away0,
+    lane1, lane0, chunk_lane1, home1, home0, away1, away0,
     part, from_z, part_z, from_plane,
     in_sem, send_sems, recv_sems,
 ):
@@ -135,7 +170,7 @@
     inner = [((x + dx) % 4) * 2 + (c + dc) % 2 for dx in (2, 1, 3, 0) for dc in (0, 1)]
     tiers = [((y + dy) % 4) * 8 for dy in (2, 1, 3, 0)]
 
-    def to_all(act, begin=0, end=8):
+    def to_all(act):
         def body(step, carry):
             dz = jnp.where(step % 2 == 0, 4 + step // 2, 4 - (step + 1) // 2)
             base = ((z + dz) % 8) * 32
@@ -144,9 +179,8 @@
                     act(base + tier + spot)
             return carry
 
-        lax.fori_loop(begin, min(end, 7), body, 0)
-        if end == 8:
-            to_plane(lambda d, spot: act(d))
+        lax.fori_loop(0, 7, body, 0)
+        to_plane(lambda d, spot: act(d))
 
     def to_plane(act):
         for t, tier in enumerate(tiers):
@@ -173,11 +207,11 @@
         row = slice(layer * 24 + q, layer * 24 + q + 1)
         return cos_tab[row, :], sy_tab[row, :], sz_tab[row, :]
 
-    def kron(out_bits, in_bits, z_bits, layer, qubits, shape):
-        real, imag = None, None
-        for position, q in enumerate(qubits):
+    def kron(value, out_bits, in_bits, layer, qubits):
+        real, imag = value
+        for position, q in qubits:
             cosine, sy, sz = coefs(layer, q)
-            if shape[1] > 128:
+            if out_bits.shape[1] > 128:
                 cosine, sy, sz = (jnp.concatenate([v, v], axis=1) for v in (cosine, sy, sz))
             b_out = (out_bits >> position) & 1
             b_in = (in_bits >> position) & 1
@@ -193,18 +227,30 @@
     def build_lane(ref, layer):
         j = lax.broadcasted_iota(jnp.int32, (128, 128), 0)
         k = lax.broadcasted_iota(jnp.int32, (128, 128), 1)
-        real, imag = kron(k, j, k, layer, LANE_QUBITS, (128, 128))
+        real, imag = kron((None, None), k, j, layer, list(enumerate(LANE_QUBITS)))
         for i, (re, im) in enumerate(zip(cut(real), cut(imag))):
             ref[i, 0:128, 0:128] = re
             ref[i, 128:256, 128:256] = re
             ref[i, 0:128, 128:256] = im
             ref[i, 128:256, 0:128] = -im
 
+    def build_chunk_lane(ref, layer):
+        j = lax.broadcasted_iota(jnp.int32, (128, 128), 0)
+        k = lax.broadcasted_iota(jnp.int32, (128, 128), 1)
+        qubits = [(p, q) for p, q in enumerate(LANE_QUBITS) if p != 4]
+        real, imag = kron((None, None), k, j, layer, qubits)
+        part_in, part_out = (j >> 4) & 1, (k >> 4) & 1
+        mixed = jnp.where(part_in == part_out, real, jnp.where(part_out == 1, imag, -imag))
+        ref[0], ref[1] = cut(mixed)
+
     def build_rows(ref, layer, qubits):
+        places = list(enumerate(qubits))
+        j = lax.broadcasted_iota(jnp.int32, (32, 256), 0)
+        k = lax.broadcasted_iota(jnp.int32, (32, 256), 1)
+        base = kron((None, None), j, k, layer, places[:5])
+
         def body(block, carry):
-            j = lax.broadcasted_iota(jnp.int32, (32, 256), 0) + block * 32
-            k = lax.broadcasted_iota(jnp.int32, (32, 256), 1)
-            real, imag = kron(j, k, j, layer, qubits, (32, 256))
+            real, imag = kron(base, j + block * 32, k, layer, places[5:])
             at = pl.ds(pl.multiple_of(block * 32, 32), 32)
             for i, (re, im) in enumerate(zip(cut(real), cut(imag))):
                 ref[0, i, at, :] = re
@@ -221,18 +267,29 @@
         a, b = mm((ref[0, 0], ref[0, 1]), x), mm((ref[1, 0], ref[1, 1]), x)
         return jnp.concatenate([a[:, :128] - b[:, 128:], a[:, 128:] + b[:, :128]], axis=1)
 
+    def apply_chunk_rows(x, ref):
+        x = cut(x)
+        return mm((ref[0, 0], ref[0, 1]), x) + times_i(mm((ref[1, 0], ref[1, 1]), x))
+
     def split(x):
         return x[:, :128], x[:, 128:]
 
     for copy in loads:
         copy.wait()
     for i in range(3):
-        send1[i] = repack(raw[i])
-    recv1[:, pl.ds(me, 1), :] = send1[:, pl.ds(me, 1), :]
+        raw[i] = repack(raw[i])
+    send_a[0], send_b[0] = to_chunks(raw[0], raw[1])
+    send_a[1] = raw[2]
+
+    def keep_own(source, target):
+        target[:, pl.ds(me, 1), :] = source[:, pl.ds(me, 1), :]
+
+    keep_own(send_a, recv_a)
+    keep_own(send_b, recv_b)
 
     pl.semaphore_wait(barrier, 255)
 
-    def exchange(source, target, slot, begin=0, end=8):
+    def exchange(source, target, slot):
         def act(d):
             pltpu.make_async_remote_copy(
                 src_ref=source.at[:, pl.ds(d, 1), :],
@@ -243,7 +300,7 @@
                 device_id_type=MESH,
             ).start()
 
-        to_all(act, begin, end)
+        to_all(act)
 
     def exchanged(source, target, slot):
         return pltpu.make_async_remote_copy(
@@ -255,8 +312,10 @@
             device_id_type=MESH,
         )
 
-    exchange(send1, recv1, 0)
-    first = exchanged(send1, recv1, 0)
+    exchange(send_a, recv_a, 0)
+    exchange(send_b, recv_b, 1)
+    out_a = exchanged(send_a, recv_a, 0)
+    out_b = exchanged(send_b, recv_b, 1)
 
     for copy in settings:
         copy.wait()
@@ -279,17 +338,13 @@
     sy_tab[...] = jnp.where(is_z, 0.0, sines)
     sz_tab[...] = jnp.where(is_z, sines, 0.0)
 
-    build_lane(lane1, 1)
+    build_chunk_lane(chunk_lane1, 1)
     build_rows(away1, 1, AWAY_ROWS)
     build_rows(away0, 0, AWAY_ROWS)
+    build_lane(lane1, 1)
     build_rows(home1, 1, HOME_ROWS)
 
     scale = 2.0 / math.sqrt(1 << QUBITS)
-
-    def start_state(ref, sign):
-        ket_re, ket_im = ref[0] * sign, ref[1] * sign
-        obs = ref[2] * scale
-        return (obs * ket_re, obs * ket_im), (ket_re, ket_im)
 
     acc = {(layer, k): jnp.zeros((8, 128), F32) for layer in range(2) for k in range(3)}
 
@@ -302,65 +357,90 @@
 
     spots = [(1, p) for p in range(7)] + [(0, p) for p in range(8)]
     local = list(LANE_QUBITS) + list(HOME_ROWS)
-    bra, ket = start_state(send1, entangle(me, False, ALL_PAIRS))
-    tally(1, local, terms(bra, ket, spots))
-    local_sign = entangle(me, False, LOCAL_PAIRS)
+    sign = entangle(me, ALL_PAIRS)
+    ket = (raw[0] * sign, raw[1] * sign)
+    bra = tuple(raw[2] * scale * part for part in ket)
+    tally(1, local, home_terms(bra, ket, spots))
+    local_sign = entangle(me, LOCAL_PAIRS)
     sign2 = jnp.concatenate([local_sign, local_sign], axis=1)
 
-    def layer_one(state, rows_ref, sign2):
+    def home_layer(state):
         x = jnp.concatenate(state, axis=1)
-        return apply_rows(apply_lanes(x, lane1), rows_ref) * sign2
-
-    bra1 = split(layer_one(bra, home1, sign2))
-    ket1 = split(layer_one(ket, home1, sign2))
+        return split(apply_rows(apply_lanes(x, lane1), home1) * sign2)
+
     inside = [(q, s) for q, s in zip(local, spots) if q not in (0, 14)]
-    tally(0, [q for q, _ in inside], terms(bra1, ket1, [s for _, s in inside]))
-
+    tally(0, [q for q, _ in inside], home_terms(home_layer(bra), home_layer(ket), [s for _, s in inside]))
+
+    def give_sums():
+        lane8 = lax.broadcasted_iota(jnp.int32, (8, 128), 1)
+        mine = jnp.zeros((8, 128), F32)
+        for layer in range(2):
+            for k in range(3):
+                value = 0.5 * jnp.sum(acc[layer, k], keepdims=True)
+                mine = mine + jnp.where(lane8 == 3 * layer + k, value, 0.0)
+        part[...] = mine
+        from_plane[pl.ds(plane, 1)] = mine[None]
+
+        def hand_over(d, spot):
+            pltpu.make_async_remote_copy(
+                src_ref=part, dst_ref=from_plane.at[plane], send_sem=send_sems.at[4], recv_sem=recv_sems.at[4],
+                device_id=(d,), device_id_type=MESH,
+            ).start()
+
+        to_plane(hand_over)
+
+    row_spots = [(0, p) for p in range(8)]
+
+    def visit(chunk, arrived, source, send, recv, slot):
+        start_sign = entangle(me, ALL_PAIRS, chunk)
+        away_sign = entangle(me, AWAY_PAIRS, chunk)
+        arrived.wait_recv()
+        obs = recv_a[1]
+        keep = lane_bit4()
+        obs = jnp.where(keep, obs, up(obs)) if chunk == 0 else jnp.where(keep, down(obs), obs)
+        ket = source[0] * start_sign
+        bra = obs * scale * ket
+
+        def away_layer(x):
+            x = mm(cut(x), (chunk_lane1[0], chunk_lane1[1]))
+            return apply_chunk_rows(x, away1) * away_sign
+
+        def leave(bra_x):
+            send[0] = apply_chunk_rows(bra_x, away0)
+            keep_own(send, recv)
+            exchange(send, recv, slot)
+
+        def take_terms(bra_x, ket_x):
+            tally(1, AWAY_ROWS, chunk_terms(bra, ket, row_spots))
+            tally(0, list(AWAY_ROWS) + [0, 14], chunk_terms(bra_x, ket_x, row_spots + [(1, 0), (1, 6)]))
+
+        if chunk == 0:
+            bra_x = away_layer(bra)
+            leave(bra_x)
+            take_terms(bra_x, away_layer(ket))
+        else:
+            x = jnp.concatenate([bra, ket], axis=0)
+            x = mm(cut(x), (chunk_lane1[0], chunk_lane1[1]))
+            x = cut(jnp.concatenate([x[:256], x[256:]], axis=1))
+            a, b = mm((away1[0, 0], away1[0, 1]), x), mm((away1[1, 0], away1[1, 1]), x)
+            bra_x = (a[:, :128] + times_i(b[:, :128])) * away_sign
+            ket_x = (a[:, 128:] + times_i(b[:, 128:])) * away_sign
+            take_terms(bra_x, ket_x)
+            give_sums()
+            leave(bra_x)
+
+    visit(0, out_a, recv_a, send_c, recv_c, 2)
+    out_c = exchanged(send_c, recv_c, 2)
+    visit(1, out_b, recv_b, send_d, recv_d, 3)
+    out_d = exchanged(send_d, recv_d, 3)
+
+    third = pltpu.make_async_remote_copy(
+        src_ref=from_plane.at[pl.ds(0, 31)], dst_ref=from_plane.at[pl.ds(0, 31)],
+        send_sem=send_sems.at[4], recv_sem=recv_sems.at[4], device_id=(me,), device_id_type=MESH,
+    )
     build_lane(lane0, 0)
     build_rows(home0, 0, HOME_ROWS)
-    away_sign = entangle(me, True, AWAY_PAIRS)
-    away2 = jnp.concatenate([away_sign, away_sign], axis=1)
-
-    first.wait_recv()
-
-    bra, ket = start_state(recv1, entangle(me, True, ALL_PAIRS))
-    bra_x = layer_one(bra, away1, away2)
-    done = apply_rows(bra_x, away0)
-    send2[0], send2[1] = split(done)
-    recv2[:, pl.ds(me, 1), :] = send2[:, pl.ds(me, 1), :]
-    exchange(send2, recv2, 1, 0, 4)
-
-    tally(1, AWAY_ROWS, terms(bra, ket, [(0, p) for p in range(8)]))
-    ket_x = layer_one(ket, away1, away2)
-    tally(
-        0,
-        list(AWAY_ROWS) + [0, 14],
-        terms(split(bra_x), split(ket_x), [(0, p) for p in range(8)] + [(1, 0), (1, 6)]),
-    )
-
-    lane8 = lax.broadcasted_iota(jnp.int32, (8, 128), 1)
-    mine = jnp.zeros((8, 128), F32)
-    for layer in range(2):
-        for k in range(3):
-            value = 0.5 * jnp.sum(acc[layer, k], keepdims=True)
-            mine = mine + jnp.where(lane8 == 3 * layer + k, value, 0.0)
-    part[...] = mine
-    from_plane[pl.ds(plane, 1)] = mine[None]
-
-    def hand_over(d, spot):
-        pltpu.make_async_remote_copy(
-            src_ref=part, dst_ref=from_plane.at[plane], send_sem=send_sems.at[2], recv_sem=recv_sems.at[2],
-            device_id=(d,), device_id_type=MESH,
-        ).start()
-
-    to_plane(hand_over)
-    third = pltpu.make_async_remote_copy(
-        src_ref=from_plane.at[pl.ds(0, 31)], dst_ref=from_plane.at[pl.ds(0, 31)],
-        send_sem=send_sems.at[2], recv_sem=recv_sems.at[2], device_id=(me,), device_id_type=MESH,
-    )
-    exchange(send2, recv2, 1, 4, 8)
-    second = exchanged(send2, recv2, 1)
-    rest_sign = entangle(me, False, REST_PAIRS)
+    rest_sign = entangle(me, REST_PAIRS)
     rest2 = jnp.concatenate([rest_sign, rest_sign], axis=1)
 
     third.wait_recv()
@@ -369,23 +449,30 @@
     from_z[pl.ds(z, 1)] = summed[None]
     for dz in (4, 3, 5, 2, 6, 1, 7):
         pltpu.make_async_remote_copy(
-            src_ref=part_z, dst_ref=from_z.at[z], send_sem=send_sems.at[3], recv_sem=recv_sems.at[3],
+            src_ref=part_z, dst_ref=from_z.at[z], send_sem=send_sems.at[5], recv_sem=recv_sems.at[5],
             device_id=(((z + dz) % 8) * 32 + plane,), device_id_type=MESH,
         ).start()
     fourth = pltpu.make_async_remote_copy(
         src_ref=from_z.at[pl.ds(0, 7)], dst_ref=from_z.at[pl.ds(0, 7)],
-        send_sem=send_sems.at[3], recv_sem=recv_sems.at[3], device_id=(me,), device_id_type=MESH,
+        send_sem=send_sems.at[5], recv_sem=recv_sems.at[5], device_id=(me,), device_id_type=MESH,
     )
 
-    second.wait_recv()
-    x2 = jnp.concatenate([recv2[0], recv2[1]], axis=1)
-    x2 = apply_rows(x2, home1) * rest2
+    cosine, sy, sz = coefs(1, 4)
+    out_c.wait_recv()
+    low = apply_chunk_rows(recv_c[0], home1)
+    out_d.wait_recv()
+    high = apply_chunk_rows(recv_d[0], home1)
+    low, high = (
+        cosine * low + sy * high + sz * times_i(low),
+        cosine * high - sy * low - sz * times_i(high),
+    )
+    x2 = jnp.concatenate(from_chunks(low, high), axis=1) * rest2
     x2 = apply_rows(apply_lanes(x2, lane0), home0)
     bra_ref[0], bra_ref[1] = split(x2)
 
     fourth.wait_recv()
     grads_ref[...] = jnp.sum(from_z[...], axis=0)
-    for copy in (first, second, third, fourth):
+    for copy in (out_a, out_b, out_c, out_d, third, fourth):
         copy.wait_send()
 
 
@@ -418,15 +505,16 @@
         out_specs=(on_chip, on_chip),
         scratch_shapes=[
             pltpu.SMEM((2, 3), F32), pltpu.SMEM((2, 32), jnp.int32),
-            vmem(3, 256, 128), vmem(3, 256, 128), vmem(3, 256, 128),
-            vmem(2, 256, 128), vmem(2, 256, 128),
+            vmem(3, 256, 128),
+            vmem(2, 256, 128), vmem(1, 256, 128), vmem(2, 256, 128), vmem(1, 256, 128),
+            vmem(1, 256, 128), vmem(1, 256, 128), vmem(1, 256, 128), vmem(1, 256, 128),
             vmem(48, 128), vmem(48, 128, dtype=jnp.int32),
             vmem(48, 128), vmem(48, 128), vmem(48, 128),
-            half(2, 256, 256), half(2, 256, 256),
+            half(2, 256, 256), half(2, 256, 256), half(2, 128, 128),
             half(2, 2, 256, 256), half(2, 2, 256, 256), half(2, 2, 256, 256), half(2, 2, 256, 256),
             vmem(8, 128), vmem(8, 8, 128), vmem(8, 128), vmem(32, 8, 128),
             pltpu.SemaphoreType.DMA((5,)),
-            pltpu.SemaphoreType.DMA((4,)), pltpu.SemaphoreType.DMA((4,)),
+            pltpu.SemaphoreType.DMA((6,)), pltpu.SemaphoreType.DMA((6,)),
         ],
         compiler_params=pltpu.CompilerParams(
             collective_id=0, has_side_effects=True, vmem_limit_bytes=16 << 20

time: 41.6 us -> 40.1 us (0.964)
  Pallas kernels: 40.9 us -> 39.4 us
    pallas_call x1, Pallas kernels: 39.3 us -> 37.8 us  [on_device(): pl.pallas_call(kernel, out_shape=(jax.ShapeDtypeStruct((2, 256, 128), F32...]
where the time goes in v2:
time: 40.1 us; the launch traced here: 40 us
  Pallas kernels  39.4 us (98%)
  between operations  0.64 us (2%)
    pallas_call x1, Pallas kernels, on_device(): pl.pallas_call(kernel, out_shape=(jax.ShapeDtypeStruct((2, 256, 128), F32...  37.8 us
    pallas_call x1, Pallas kernels, on_device(): pl.pallas_call(finish, out_shape=(jax.ShapeDtypeStruct((256, 2, 128), F32...  1.54 us

profile of v2, /device:TPU:1, one launch (start us, length us, event | category | flops | bytes accessed | tf_op | source)
XLA Modules:
  0.0 40.0 jit_solution(10271280227407170412)
XLA Ops:
  0.6 37.8 %shard_map.59 = (f32[2,256,128]{2,1,0:T(8,128)S(1)}, f32[8,128]{1,0:T(8,128)S(1)}) custom-call(f32[256,2,128]{2,1,0:T(2,128)} %bitcast.7, f32[256,128]{1,0:T(8,128)} %bitcast.8, f32[2,3]{1,0:T(2,128)} %angles_hbm.1, s32[2,32]{1,0:T(2,128)} %kinds_hbm.1), custom_call_target="tpu_custom_call" | custom-call | tf_op jit(solution)/shard_map/pallas_call | solution.py:498
  38.5 1.5 %shard_map.60 = (f32[256,2,128]{2,1,0:T(2,128)}, f32[2,3]{1,0:T(2,128)}) custom-call(f32[2,256,128]{2,1,0:T(8,128)S(1)} %get-tuple-element.6.state, f32[8,128]{1,0:T(8,128)S(1)} %get-tuple-element.7.sums), custom_call_target="tpu_custom_call" | custom-call | tf_op jit(solution)/shard_map/pallas_call | solution.py:523

commit v3 on v2

--- a/solution.py
+++ b/solution.py
@@ -477,15 +477,13 @@
 
 
 def finish(state, sums, bra_hbm, grads_ref, raw, out_sem):
-    stores = []
     for i in range(2):
-        raw[i] = repack(state[i])
-        stores.append(pltpu.make_async_copy(raw.at[i], bra_hbm.at[:, i, :], out_sem.at[i]))
-        stores[i].start()
+        raw[pl.ds(i, 256, 2), :] = repack(state[i])
+    store = pltpu.make_async_copy(raw, bra_hbm, out_sem)
+    store.start()
     total = sums[0:1, :]
     grads_ref[...] = jnp.concatenate([total[:, 0:3], total[:, 3:6]], axis=0)
-    for copy in stores:
-        copy.wait()
+    store.wait()
 
 
 def on_device(ket_state, observable, angles, gate_kinds):
@@ -523,15 +521,15 @@
     bra, grads = pl.pallas_call(
         finish,
         out_shape=(
-            jax.ShapeDtypeStruct((256, 2, 128), F32),
+            jax.ShapeDtypeStruct((512, 128), F32),
             jax.ShapeDtypeStruct((2, 3), F32),
         ),
         in_specs=[on_chip, on_chip],
         out_specs=(main_memory, on_chip),
-        scratch_shapes=[vmem(2, 256, 128), pltpu.SemaphoreType.DMA((2,))],
+        scratch_shapes=[vmem(512, 128), pltpu.SemaphoreType.DMA(())],
         compiler_params=pltpu.CompilerParams(vmem_limit_bytes=4 << 20),
     )(state, sums)
-    return bra.transpose(1, 0, 2).reshape(2, 32768), grads
+    return bra.reshape(256, 2, 128).transpose(1, 0, 2).reshape(2, 32768), grads
 
 
 def solution(mesh):

time: 40.1 us -> 40.1 us (level)
  no operation moved by 1% of the time
where the time goes in v3:
time: 40.1 us; the launch traced here: 40 us
  Pallas kernels  39.4 us (98%)
  between operations  0.64 us (2%)
    pallas_call x1, Pallas kernels, on_device(): pl.pallas_call(kernel, out_shape=(jax.ShapeDtypeStruct((2, 256, 128), F32...  37.8 us
    pallas_call x1, Pallas kernels, on_device(): pl.pallas_call(finish, out_shape=(jax.ShapeDtypeStruct((512, 128), F32),...  1.57 us

profile of v3, /device:TPU:1, one launch (start us, length us, event | category | flops | bytes accessed | tf_op | source)
XLA Modules:
  0.0 40.0 jit_solution(2020344477741572470)
XLA Ops:
  0.6 37.8 %shard_map.59 = (f32[2,256,128]{2,1,0:T(8,128)S(1)}, f32[8,128]{1,0:T(8,128)S(1)}) custom-call(f32[256,2,128]{2,1,0:T(2,128)} %bitcast.9, f32[256,128]{1,0:T(8,128)} %bitcast.10, f32[2,3]{1,0:T(2,128)} %angles_hbm.1, s32[2,32]{1,0:T(2,128)} %kinds_hbm.1), custom_call_target="tpu_custom_call" | custom-call | tf_op jit(solution)/shard_map/pallas_call | solution.py:496
  38.5 1.6 %shard_map.60 = (f32[512,128]{1,0:T(8,128)}, f32[2,3]{1,0:T(2,128)}) custom-call(f32[2,256,128]{2,1,0:T(8,128)S(1)} %get-tuple-element.6.state, f32[8,128]{1,0:T(8,128)S(1)} %get-tuple-element.7.sums), custom_call_target="tpu_custom_call" | custom-call | tf_op jit(solution)/shard_map/pallas_call | solution.py:521

commit v4 on v2

--- a/solution.py
+++ b/solution.py
@@ -170,17 +170,20 @@
     inner = [((x + dx) % 4) * 2 + (c + dc) % 2 for dx in (2, 1, 3, 0) for dc in (0, 1)]
     tiers = [((y + dy) % 4) * 8 for dy in (2, 1, 3, 0)]
 
+    columns = [((z + dz) % 8) * 32 for dz in (4, 3, 5, 2, 6, 1, 7, 0)]
+
     def to_all(act):
         def body(step, carry):
-            dz = jnp.where(step % 2 == 0, 4 + step // 2, 4 - (step + 1) // 2)
-            base = ((z + dz) % 8) * 32
-            for tier in tiers:
-                for spot in inner:
-                    act(base + tier + spot)
+            dy, dx, dc = step // 8 + 2, (step // 2) % 4 + 2, step % 2
+            spot = ((y + dy) % 4) * 8 + ((x + dx) % 4) * 2 + (c + dc) % 2
+            for column in columns:
+                act(column + spot)
             return carry
 
-        lax.fori_loop(0, 7, body, 0)
-        to_plane(lambda d, spot: act(d))
+        lax.fori_loop(0, 20, body, 0)
+        lax.fori_loop(21, 32, body, 0)
+        for column in columns[:7]:
+            act(column + plane)
 
     def to_plane(act):
         for t, tier in enumerate(tiers):
@@ -394,12 +397,16 @@
     def visit(chunk, arrived, source, send, recv, slot):
         start_sign = entangle(me, ALL_PAIRS, chunk)
         away_sign = entangle(me, AWAY_PAIRS, chunk)
-        arrived.wait_recv()
+        if chunk == 0:
+            arrived.wait_recv()
         obs = recv_a[1]
         keep = lane_bit4()
         obs = jnp.where(keep, obs, up(obs)) if chunk == 0 else jnp.where(keep, down(obs), obs)
+        obs = obs * scale
+        if chunk == 1:
+            arrived.wait_recv()
         ket = source[0] * start_sign
-        bra = obs * scale * ket
+        bra = obs * ket
 
         def away_layer(x):
             x = mm(cut(x), (chunk_lane1[0], chunk_lane1[1]))

time: 40.1 us -> 41.5 us (1.035)
  Pallas kernels: 39.4 us -> 40.7 us
    pallas_call x1, Pallas kernels: 37.8 us -> 39.2 us  [on_device(): pl.pallas_call(kernel, out_shape=(jax.ShapeDtypeStruct((2, 256, 128), F32...]
where the time goes in v4:
time: 41.5 us; the launch traced here: 41.4 us
  Pallas kernels  40.7 us (98%)
  between operations  0.64 us (2%)
    pallas_call x1, Pallas kernels, on_device(): pl.pallas_call(kernel, out_shape=(jax.ShapeDtypeStruct((2, 256, 128), F32...  39.2 us
    pallas_call x1, Pallas kernels, on_device(): pl.pallas_call(finish, out_shape=(jax.ShapeDtypeStruct((256, 2, 128), F32...  1.54 us

profile of v4, /device:TPU:1, one launch (start us, length us, event | category | flops | bytes accessed | tf_op | source)
XLA Modules:
  0.0 41.4 jit_solution(14993891260509107867)
XLA Ops:
  0.6 39.2 %shard_map.59 = (f32[2,256,128]{2,1,0:T(8,128)S(1)}, f32[8,128]{1,0:T(8,128)S(1)}) custom-call(f32[256,2,128]{2,1,0:T(2,128)} %bitcast.7, f32[256,128]{1,0:T(8,128)} %bitcast.8, f32[2,3]{1,0:T(2,128)} %angles_hbm.1, s32[2,32]{1,0:T(2,128)} %kinds_hbm.1), custom_call_target="tpu_custom_call" | custom-call | tf_op jit(solution)/shard_map/pallas_call | solution.py:505
  39.8 1.5 %shard_map.60 = (f32[256,2,128]{2,1,0:T(2,128)}, f32[2,3]{1,0:T(2,128)}) custom-call(f32[2,256,128]{2,1,0:T(8,128)S(1)} %get-tuple-element.6.state, f32[8,128]{1,0:T(8,128)S(1)} %get-tuple-element.7.sums), custom_call_target="tpu_custom_call" | custom-call | tf_op jit(solution)/shard_map/pallas_call | solution.py:530
